TPU v7x, 128 devices: a whole 4x4x4 slice. The times are simulated.
128 devices in a mesh: row: 8 (over z, y_hi), col: 16 (over y_lo, x, core).
Axes of the slice: x: 4, y: 4 (y_hi: 2, y_lo: 2; y = y_hi * 2 + y_lo), z: 4, core: 2. Of those that a mesh axis runs over, the one named last changes fastest.
Arguments:
- operator: bfloat16 [32768, 32768], P('row', 'col'), may hold values from -6 to 6
- right_test: bfloat16 [32768, 256], P('col'), may hold values from -0.03125 to 0.03125
- left_test: bfloat16 [32768, 384], P('row'), may hold values from -0.03125 to 0.03125
Outputs:
- left_factor: bfloat16 [32768, 256], P(('row', 'col'))
- right_factor: bfloat16 [32768, 256], P('col')
All inputs are finite; a program needn't handle non-finite values.
Results may differ from a plain program's by a relative error of at most 0.0015.
Values may be sent and summed in bfloat16 or wider, within the bound.
A program may use at most 128 MiB of HBM per device.

v0:
```python
import jax
import jax.numpy as jnp
from jax import lax
from jax.sharding import PartitionSpec as P


def joined_along(tiles, dim):
    shape = list(tiles.shape[1:])
    shape[dim] *= tiles.shape[0]
    return jnp.moveaxis(tiles, 0, dim).reshape(shape)


def from_everyone(value, axis):
    copies = jnp.broadcast_to(value, (lax.axis_size(axis), *value.shape))
    return lax.all_to_all(copies, axis, split_axis=0, concat_axis=0, tiled=True)


def collect(value, axis, dim):
    return joined_along(from_everyone(value, axis), dim)


def body(operator, right_test, left_test):
    width_right = right_test.shape[1]
    block_left = jnp.dot(operator, right_test, preferred_element_type=jnp.float32)
    block_core = lax.dot_general(
        left_test.astype(jnp.float32),
        block_left,
        (((0,), (0,)), ((), ())),
        precision=lax.Precision.HIGHEST,
    )
    core_matrix = lax.psum(block_core, ("row", "col"))
    left_share = lax.psum_scatter(block_left, "col", scatter_dimension=0, tiled=True)
    right_share = lax.psum_scatter(
        lax.dot_general(
            operator, left_test, (((0,), (0,)), ((), ())), preferred_element_type=jnp.float32
        ),
        "row",
        scatter_dimension=0,
        tiled=True,
    )
    gram_plain = jnp.dot(core_matrix.T, core_matrix, precision=lax.Precision.HIGHEST)
    shift_size = 0.001 * jnp.trace(gram_plain) / width_right
    gram_matrix = gram_plain + shift_size * jnp.eye(width_right, dtype=jnp.float32)
    lower_factor = jnp.linalg.cholesky(gram_matrix)
    solve_map = jax.scipy.linalg.cho_solve((lower_factor, True), core_matrix.T)
    factor_share = jnp.dot(right_share, solve_map.T, precision=lax.Precision.HIGHEST).astype(
        jnp.bfloat16
    )
    right_factor = collect(factor_share, "row", 0)
    return (left_share.astype(jnp.bfloat16), right_factor)


def solution(mesh):
    placed = (P("row", "col"), P("col", None), P("row", None))
    return jax.shard_map(
        body,
        mesh=mesh,
        in_specs=placed,
        out_specs=(P(("row", "col"), None), P("col", None)),
        check_vma=False,
    )
```

profile of v0, /device:TPU:0, one launch (start us, length us, event | category | flops | bytes accessed | tf_op | source)
XLA Modules:
  0.0 306.5 jit_solution(8968853385151517210)
XLA Ops:
  8.0 0.0 copy-start
  8.0 0.0 all-reduce.3.cloned.1.call-start
  8.1 12.6 %fusion.17 = f32[4096,256]{1,0:T(8,128)} fusion(bf16[4096,2048]{1,0:T(8,128)(2,1)} %param.3, bf16[2048,256]{1,0:T(8,128)(2,1)} %param.4), kind=kOutput, calls=%fused_computation.42 | convolution fusion | flops 4294967296 | bytes 22020096 | tf_op jit(solution)/shard_map/dot_general | solution.py:24
  20.7 0.0 copy-done
  20.7 6.4 %convolution_bitcast_fusion = f32[384,256]{0,1:T(8,128)} fusion(f32[4096,256]{1,0:T(8,128)} %fusion.17, bf16[4096,384]{1,0:T(8,128)(2,1)S(1)} %copy-done), kind=kOutput, calls=%fused_computation.2 | convolution fusion | flops 4831838208 | bytes 7733248 | tf_op jit(solution)/shard_map/dot_general | solution.py:25
  27.1 0.0 all-reduce.3.cloned.1.call-update
  27.1 0.0 reduce-scatter.5.cloned.1.call-start
  27.2 13.6 %fusion.18 = f32[2048,384]{1,0:T(8,128)} fusion(bf16[4096,2048]{1,0:T(8,128)(2,1)} %param.3, bf16[4096,384]{1,0:T(8,128)(2,1)S(1)} %copy-done), kind=kOutput, calls=%fused_computation.43 | convolution fusion | flops 6442450944 | bytes 23068672 | tf_op jit(solution)/shard_map/dot_general | solution.py:34
  40.8 0.0 reduce-scatter.5.cloned.1.call-update
  40.8 0.2 reduce-scatter.3.cloned.1.call-start
  41.0 0.4 reduce-scatter.3.cloned.1.call-update
  41.4 137.6 %all-reduce.3.cloned.1.call-done = f32[384,256]{0,1:T(8,128)} async-done(((f32[384,256]{0,1:T(8,128)}), f32[384,256]{0,1:T(8,128)}) %all-reduce.3.cloned.1.call-update) | async-done | bytes 393232 | tf_op jit(solution)/shard_map/psum | solution.py:31
  179.0 3.1 %select_reduce_fusion = (f32[]{:T(128)}, f32[256,256]{1,0:T(8,128)}) fusion(f32[384,256]{0,1:T(8,128)} %all-reduce.3.cloned.1.call-done), kind=kOutput, calls=%fused_computation.15 | convolution fusion | flops 302186496 | bytes 655364 | tf_op jit(solution)/shard_map/dot_general | solution.py:41
  182.1 1.8 copy.5
  184.5 1.1 fusion.4
  185.6 0.0 copy-start.2
  185.6 0.7 copy-done.2
  186.3 0.6 cholesky.115
  187.0 13.2 %cholesky.49 = f32[128,128]{1,0:T(8,128)} custom-call(f32[128,128]{1,0:T(8,128)} %cholesky.115), custom_call_target="Cholesky" | custom-call | tf_op jit(solution)/shard_map/jit(cholesky)/cholesky | solution.py:44
  200.1 1.5 select_reduce_fusion.2
  201.6 11.3 %custom-call.18 = f32[1,128,128]{1,2,0:T(8,128)} custom-call(f32[1,128,128]{2,1,0:T(8,128)} %get-tuple-element.23), custom_call_target="InvertDiagBlocksLowerTriangular" | custom-call | tf_op jit(solution)/shard_map/jit(cholesky)/cholesky | solution.py:44
  212.9 1.6 cholesky.111
  214.4 1.7 constant_dynamic-update-slice_fusion.1
  216.1 1.7 convolution_subtract_fusion.2
  217.9 13.2 %cholesky.103 = f32[128,128]{1,0:T(8,128)} custom-call(f32[128,128]{1,0:T(8,128)} %convolution_subtract_fusion.2), custom_call_target="Cholesky" | custom-call | tf_op jit(solution)/shard_map/jit(cholesky)/cholesky | solution.py:44
  231.0 1.5 select_reduce_fusion.1
  232.5 0.7 compare_reduce_fusion
  234.4 1.7 select_select_fusion
  236.1 0.1 triangular_solve.74
  236.1 6.7 %while.1 = (s32[]{:T(128)}, f32[256,256]{1,0:T(8,128)}, s32[2,2]{1,0:T(2,128)S(1)}, f32[2,128,128]{2,1,0:T(8,128)}, s32[]{:T(128)}) while((s32[]{:T(128)}, f32[256,256]{1,0:T(8,128)}, s32[2,2]{1,0:T(2,128)S(1)}, f32[2,128,128]{2,1,0:T(8,128)}, s32[]{:T(128)}) %tuple.28), condition=%wide.while_cond, body=%wide.while_body.sunk | while | flops 2 | bytes 132205 | solution.py:45
  236.1 0.6 fusion.36
  236.7 2.8 bitcast_dynamic-update-slice_fusion.2
  239.5 0.6 fusion.36
  240.1 2.8 bitcast_dynamic-update-slice_fusion.2
  242.9 21.1 %custom-call.19 = f32[2,128,128]{1,2,0:T(8,128)} custom-call(f32[2,128,128]{2,1,0:T(8,128)} %get-tuple-element.9), custom_call_target="InvertDiagBlocksLowerTriangular" | custom-call | tf_op jit(solution)/shard_map/jit(_cho_solve)/triangular_solve | solution.py:45
  263.9 0.0 copy-done.1
  263.9 1.2 fusion.5
  265.2 1.2 convolution_subtract_fusion.1
  266.3 1.2 fusion.12
  267.5 1.2 fusion.11
  268.7 1.2 convolution_subtract_fusion
  269.9 1.2 fusion.10
  271.1 0.0 reduce-scatter.5.cloned.1.call-done
  271.1 1.6 convolution_convert_fusion
  272.7 0.1 broadcast_in_dim.10
  272.8 22.3 %all_to_all.5 = bf16[8,256,256]{2,1,0:T(8,128)(2,1)} all-to-all(bf16[8,256,256]{2,1,0:T(8,128)(2,1)S(1)} %broadcast_in_dim.10), channel_id=1, replica_groups=mesh['row'=8,'col'=16] {'row'}, dimensions={0} | all-to-all | bytes 2097152 | tf_op jit(solution)/shard_map/all_to_all | solution.py:15
  295.2 1.6 convert_element_type.8
  296.8 2.3 copy.19
  (6 shorter events, 0.0 us)
Async XLA Ops:
  8.0 12.7 %copy-start = (bf16[4096,384]{1,0:T(8,128)(2,1)S(1)}, bf16[4096,384]{1,0:T(8,128)(2,1)}, u32[]{:S(2)}) copy-start(bf16[4096,384]{1,0:T(8,128)(2,1)} %param.5) | copy-start | bytes 9437188
  8.0 171.0 %all-reduce.3.cloned.1.call-start = ((), (), s32[]{:S(2)}) async-start(), calls=%async_computation.5 | async-start | bytes 786432 | tf_op jit(solution)/shard_map/psum | solution.py:31
  27.1 244.0 %reduce-scatter.5.cloned.1.call-start = ((), (), s32[]{:S(2)}) async-start(), calls=%async_computation.4 | async-start | bytes 3538944 | tf_op jit(solution)/shard_map/reduce_scatter | solution.py:33
  40.8 254.3 %reduce-scatter.3.cloned.1.call-start = ((), (), s32[]{:S(2)}) async-start(), calls=%async_computation.3 | async-start | bytes 4456448 | tf_op jit(solution)/shard_map/reduce_scatter | solution.py:32
  179.0 85.0 %copy-start.1 = (f32[384,256]{0,1:T(8,128)S(1)}, f32[384,256]{0,1:T(8,128)}, u32[]{:S(2)}) copy-start(f32[384,256]{0,1:T(8,128)} %all-reduce.3.cloned.1.call-done) | copy-start | bytes 1179652
  185.6 0.7 copy-start.2
Sparse Core Ops, SparseCore 0:
  27.2 151.7 all-reduce.2
Sparse Core Ops, SparseCore 1:
  40.9 82.6 reduce-scatter.4
  125.8 66.2 reduce-scatter.2
where the time goes:
time: 308 us; the launch traced here: 306 us
  waiting for transfers between devices  138 us (45%)
  other arithmetic  66.7 us (22%)
  matrix products  47.9 us (16%)
  blocking collectives  22.3 us (7%)
  between operations  17.4 us (6%)
  local copies, waits for them, and re-layouts  13.8 us (4%)
    psum x1, waiting for transfers between devices, body(): core_matrix = lax.psum(block_core, ('row', 'col'))  138 us
    another operation x6, other arithmetic, body(): lower_factor = jnp.linalg.cholesky(gram_matrix)  41.2 us
    another operation x3, other arithmetic, body(): solve_map = jax.scipy.linalg.cho_solve((lower_factor, True), core_matrix.T)  22.8 us
    all_to_all x1, blocking collectives, from_everyone(): return lax.all_to_all(copies, axis, split_axis=0, concat_axis=0, tiled=True)  22.3 us
    dot_general x1, matrix products, body(): lax.dot_general(operator, left_test, (((0,), (0,)), ((), ())), preferred_...  13.6 us
    dot_general x1, matrix products, body(): jnp.dot(operator, right_test, preferred_element_type=jnp.float32)  12.6 us
    another operation x6, matrix products, body(): solve_map = jax.scipy.linalg.cho_solve((lower_factor, True), core_matrix.T)  7.09 us
    another operation x6, local copies, waits for them, and re-layouts  6.71 us
  transfers between devices with their start and end apart: 3, of which 1 were waited for; matrix products, arithmetic and copies ran while one was open for 34% of the time, Pallas kernels for 0%

commit v1 on v0

v1 whole, which is shorter than its diff:
```python
import jax
import jax.numpy as jnp
from jax import lax
from jax.experimental import pallas as pl
from jax.experimental.pallas import tpu as pltpu
from jax.sharding import PartitionSpec as P

MESH = pl.DeviceIdType.MESH
F32 = jnp.float32
BF16 = jnp.bfloat16
HIGHEST = lax.Precision.HIGHEST
SCALE_ROWS = 16
TOP = 2.0**15


def dot(a, b, dims=((1,), (0,)), precision=None):
    return lax.dot_general(a, b, (dims, ((), ())), precision=precision, preferred_element_type=F32)


def largest(value):
    return jnp.maximum(jnp.max(jnp.abs(value), axis=(0, 1), keepdims=True), 1e-30)


def store_coded(ref, value):
    rows, columns = value.shape
    scale = jnp.broadcast_to(largest(value) * 1.01, (SCALE_ROWS, columns)).astype(BF16)
    ref[pl.ds(rows, SCALE_ROWS), :] = scale
    t = value * (TOP / scale.astype(F32)[0:1, :])
    t2 = t * t
    t4 = t2 * t2
    t8 = t4 * t4
    ref[pl.ds(0, rows), :] = jnp.where(t < 0, -t8, t8).astype(BF16)


def load_coded(ref, rows):
    scale = ref[pl.ds(rows, SCALE_ROWS), :].astype(F32)[0:1, :] * (1.0 / TOP)
    y = ref[pl.ds(0, rows), :].astype(F32)
    r = jnp.sqrt(jnp.sqrt(jnp.sqrt(jnp.abs(y)))) * scale
    return jnp.where(y < 0, -r, r)


def inverse_128(a):
    n = a.shape[0]
    sub = lax.broadcasted_iota(jnp.int32, (8, n), 0)
    lane8 = lax.broadcasted_iota(jnp.int32, (8, n), 1)
    lane = lax.broadcasted_iota(jnp.int32, (n, n), 1)
    for k0 in range(0, n, 8):
        p = a[k0 : k0 + 8, :]
        c = [jnp.broadcast_to(p[:, k0 + j : k0 + j + 1], (8, n)) for j in range(8)]
        for k in range(8):
            r = 1.0 / c[k][k : k + 1, :]
            ck = c[k]
            new = []
            for j in range(8):
                if j == k:
                    new.append(jnp.where(sub == k, r, -ck * r))
                else:
                    pj = c[j][k : k + 1, :] * r
                    new.append(jnp.where(sub == k, pj, c[j] - ck * pj))
            c = new
        inside8 = (lane8 >= k0) & (lane8 < k0 + 8)
        pivot = jnp.where(inside8, jnp.where(lane8 == sub + k0, 1.0, 0.0), p)
        x = c[0] * pivot[0:1, :]
        for j in range(1, 8):
            x = x + c[j] * pivot[j : j + 1, :]
        inside = (lane >= k0) & (lane < k0 + 8)
        rest = jnp.where(inside, 0.0, a)
        for j in range(8):
            rest = rest - a[:, k0 + j : k0 + j + 1] * x[j : j + 1, :]
        pieces = [rest[:k0]] * (k0 > 0) + [x] + [rest[k0 + 8 :]] * (k0 + 8 < n)
        a = jnp.concatenate(pieces, axis=0)
    return a


def inverse_256(g):
    h = g.shape[0] // 2
    a, b, d = g[:h, :h], g[:h, h:], g[h:, h:]
    ai = inverse_128(a)
    y = dot(ai, b, precision=HIGHEST)
    si = inverse_128(d - dot(b, y, ((0,), (0,)), HIGHEST))
    t = dot(y, si, precision=HIGHEST)
    top = ai + dot(t, y, ((1,), (1,)), HIGHEST)
    return jnp.concatenate(
        [jnp.concatenate([top, -t], axis=1), jnp.concatenate([-t.T, si], axis=1)], axis=0
    )


def kernel(
    a_hbm, r_hbm, l_hbm, left_out, right_out,
    a_v, r_v, l_v, lt_v, acc, lacc,
    cbuf, cd, h1, cx, h2, cy, h3, cz, g0,
    rsend, rz, rsum, ysend, ry, ag,
    ld, lsend, lr, w_hi, w_lo,
    in_sem, ss, rs,
):
    m, n = a_hbm.shape
    r1 = r_hbm.shape[1]
    r2 = l_hbm.shape[1]
    row, col = lax.axis_index("row"), lax.axis_index("col")
    z, yh = row // 2, row % 2
    yl, x, core = col // 8, (col // 2) % 4, col % 2
    y = yh * 2 + yl
    share = 256

    def dev(zz, yy, xx, cc):
        return (zz * 2 + yy // 2, (yy % 2) * 8 + xx * 2 + cc)

    chunk = m // 4
    loads = []
    for i in range(4):
        part = pl.ds(i * chunk, chunk)
        loads.append(pltpu.make_async_copy(l_hbm.at[part], l_v.at[part], in_sem.at[2 * i]))
        loads.append(pltpu.make_async_copy(a_hbm.at[part], a_v.at[part], in_sem.at[2 * i + 1]))
    loads.append(pltpu.make_async_copy(r_hbm, r_v, in_sem.at[8]))
    for load in loads:
        load.start()

    partner = dev(z, y, x, 1 - core)
    z_peers = [dev((z + k) % 4, y, x, core) for k in (1, 2, 3)]
    y_peers = [dev(z, (y + k) % 4, x, core) for k in (1, 2, 3)]
    x_peers = [dev(z, y, (x + k) % 4, core) for k in (1, 2, 3)]
    xy_peers = [dev(z, yh * 2 + 1 - yl, (x + k) % 4, core) for k in (1, 2, 3)]
    flip_yl = dev(z, yh * 2 + 1 - yl, x, core)
    flip_yh = dev(z, (1 - yh) * 2 + yl, x, core)
    barrier = pltpu.get_barrier_semaphore()
    for peer in [partner] + z_peers + y_peers + x_peers + xy_peers:
        pl.semaphore_signal(barrier, inc=1, device_id=peer, device_id_type=MESH)

    count = [0]
    started = []

    def push(src, dst, peer):
        i = count[0]
        count[0] += 1
        copy = pltpu.make_async_remote_copy(
            src_ref=src, dst_ref=dst, send_sem=ss.at[i], recv_sem=rs.at[i],
            device_id=peer, device_id_type=MESH,
        )
        copy.start()
        started.append(copy)
        return copy

    acc[...] = jnp.zeros_like(acc)

    for i in range(4):
        loads[2 * i].wait()
        lt_v[...] = l_v[pl.ds(i * chunk, chunk), :].T
        loads[2 * i + 1].wait()

        @pl.loop(0, n // 256)
        def _(t):
            here = pl.ds(pl.multiple_of(t * 256, 256), 256)
            acc[:, here] += dot(lt_v[...], a_v[pl.ds(i * chunk, chunk), here])

    loads[8].wait()
    core_part = jnp.zeros((r2, r1), F32)
    cbuf[...] = jnp.zeros_like(cbuf)

    @pl.loop(0, n // 512)
    def _(t):
        here = pl.ds(pl.multiple_of(t * 512, 512), 512)
        v = acc[:, here]
        hi = v.astype(BF16)
        v = v - hi.astype(F32)
        mid = v.astype(BF16)
        lo = (v - mid.astype(F32)).astype(BF16)
        rt = r_v[here, :]
        part = dot(hi, rt) + (dot(mid, rt) + dot(lo, rt))
        cbuf[pl.ds(0, r2), :] += part[:, :128]
        cbuf[pl.ds(r2, r2), :] += part[:, 128:]

    pl.semaphore_wait(barrier, 13)

    half = pl.multiple_of((1 - core) * r2, 8)
    c_d = push(cbuf.at[pl.ds(half, r2)], cd, partner)

    @pl.loop(0, 8)
    def _(q):
        here = pl.ds(pl.multiple_of(q * share, share), share)
        store_coded(rsend.at[q], acc[:, here])

    right_z = [
        push(rsend.at[pl.ds(((z + k) % 4) * 2, 2)], rz.at[k - 1], z_peers[k - 1]) for k in (1, 2, 3)
    ]

    c_d.wait_recv()
    h1[...] = cbuf[pl.ds(pl.multiple_of(core * r2, 8), r2), :] + cd[...]
    n1 = r2 // 4
    c_x = [
        push(h1.at[pl.ds(pl.multiple_of(((x + k) % 4) * n1, 8), n1)], cx.at[k - 1], x_peers[k - 1])
        for k in (1, 2, 3)
    ]

    @pl.loop(0, 8)
    def _(q):
        rows = pl.ds(pl.multiple_of(q * 512, 512), 512)
        part = dot(a_v[rows, :], r_v[...])
        lacc[q, 0] = part[:256]
        lacc[q, 1] = part[256:]

    left_d = push(lacc.at[:, 1 - core], ld, partner)

    for copy in c_x:
        copy.wait_recv()
    h2[...] = h1[pl.ds(pl.multiple_of(x * n1, 8), n1), :] + (cx[0] + cx[1] + cx[2])
    n2 = n1 // 4
    c_y = [
        push(h2.at[pl.ds(pl.multiple_of(((y + k) % 4) * n2, 8), n2)], cy.at[k - 1], y_peers[k - 1])
        for k in (1, 2, 3)
    ]
    for copy in c_y:
        copy.wait_recv()
    h3[...] = h2[pl.ds(pl.multiple_of(y * n2, 8), n2), :] + (cy[0] + cy[1] + cy[2])
    cz[z] = h3[...]
    c_z = [push(h3, cz.at[z], z_peers[k - 1]) for k in (1, 2, 3)]

    left_d.wait_recv()
    me_q = yl * 4 + x

    @pl.loop(0, 8)
    def _(q):
        store_coded(lsend.at[q], lacc[q, core] + ld[q])

    for copy in c_z:
        copy.wait_recv()
    base2 = pl.multiple_of(core * r2 + x * n1, 8)
    base3 = pl.multiple_of(core * r2 + x * n1 + y * n2, 8)
    g0[pl.ds(base3, n2), :] = (cz[0] + cz[1]) + (cz[2] + cz[3])
    own = g0.at[pl.ds(base3, n2)]
    g_y = [push(own, own, y_peers[k - 1]) for k in (1, 2, 3)]

    left_flip = push(lsend.at[(1 - yl) * 4 + x], lr.at[0], flip_yl)
    left_x = [push(lsend.at[yl * 4 + (x + k) % 4], lr.at[k], x_peers[k - 1]) for k in (1, 2, 3)]
    left_xy = [
        push(lsend.at[(1 - yl) * 4 + (x + k) % 4], lr.at[k + 3], xy_peers[k - 1]) for k in (1, 2, 3)
    ]

    for copy in g_y:
        copy.wait_recv()
    own = g0.at[pl.ds(base2, n1)]
    g_x = [push(own, own, x_peers[k - 1]) for k in (1, 2, 3)]

    for copy in right_z:
        copy.wait_recv()

    @pl.loop(0, 2)
    def _(h):
        here = pl.ds(pl.multiple_of((z * 2 + h) * share, share), share)
        total = acc[:, here]
        for k in range(3):
            total = total + load_coded(rz.at[k, h], r2)
        rsum[h] = total

    store_coded(ysend, rsum[1 - yh])
    right_y = push(ysend, ry, flip_yh)

    for copy in g_x:
        copy.wait_recv()
    own = g0.at[pl.ds(pl.multiple_of(core * r2, 8), r2)]
    g_d = push(own, own, partner)

    right_y.wait_recv()
    store_coded(ag.at[row], (rsum[yh] + load_coded(ry, r2)).T)
    ag_y = push(ag.at[row], ag.at[row], flip_yh)

    g_d.wait_recv()
    core_all = jnp.concatenate([g0[pl.ds(0, r2), :], g0[pl.ds(r2, r2), :]], axis=1)
    gram = dot(core_all, core_all, ((0,), (0,)), HIGHEST)
    eye = jnp.where(
        lax.broadcasted_iota(jnp.int32, (r1, r1), 0) == lax.broadcasted_iota(jnp.int32, (r1, r1), 1), 1.0, 0.0
    )
    shift = jnp.sum(gram * eye, axis=(0, 1), keepdims=True) * 0.001 / r1
    gram = gram + shift * eye

    ag_y.wait_recv()
    both = ag.at[pl.ds(z * 2, 2)]
    ag_z = [push(both, both, z_peers[k - 1]) for k in (1, 2, 3)]

    w = dot(core_all, inverse_256(gram), precision=HIGHEST)
    w_hi[...] = w.astype(BF16)
    w_lo[...] = (w - w_hi[...].astype(F32)).astype(BF16)

    for copy in [left_flip] + left_x + left_xy:
        copy.wait_recv()
    total = lacc[me_q, core] + ld[me_q]
    for k in range(7):
        total = total + load_coded(lr.at[k], share)
    left_out[...] = total.astype(BF16)

    for copy in ag_z:
        copy.wait_recv()

    @pl.loop(0, 8)
    def _(q):
        b = load_coded(ag.at[q], share)
        hi = b.astype(BF16)
        lo = (b - hi.astype(F32)).astype(BF16)
        v = dot(hi, w_hi[...]) + (dot(hi, w_lo[...]) + dot(lo, w_hi[...]))
        right_out[pl.ds(pl.multiple_of(q * share, share), share), :] = v.astype(BF16)

    for copy in started:
        copy.wait_send()


def body(operator, right_test, left_test):
    m, n = operator.shape
    r1, r2 = right_test.shape[1], left_test.shape[1]
    share = 256
    coded = SCALE_ROWS
    vmem = pltpu.VMEM
    n1, n2 = r2 // 4, r2 // 16
    copies = 40
    return pl.pallas_call(
        kernel,
        out_shape=(
            jax.ShapeDtypeStruct((share, r1), BF16),
            jax.ShapeDtypeStruct((n, r1), BF16),
        ),
        in_specs=[pl.BlockSpec(memory_space=pl.ANY)] * 3,
        out_specs=(pl.BlockSpec(memory_space=pltpu.VMEM),) * 2,
        scratch_shapes=[
            vmem((m, n), BF16), vmem((n, r1), BF16), vmem((m, r2), BF16), vmem((r2, m // 4), BF16),
            vmem((r2, n), F32), vmem((8, 2, share, r1), F32),
            vmem((2 * r2, 128), F32), vmem((r2, 128), F32), vmem((r2, 128), F32),
            vmem((3, n1, 128), F32), vmem((n1, 128), F32), vmem((3, n2, 128), F32),
            vmem((n2, 128), F32), vmem((4, n2, 128), F32), vmem((2 * r2, 128), F32),
            vmem((8, r2 + coded, share), BF16), vmem((3, 2, r2 + coded, share), BF16),
            vmem((2, r2, share), F32), vmem((r2 + coded, share), BF16), vmem((r2 + coded, share), BF16),
            vmem((8, share + coded, r2), BF16),
            vmem((8, share, r1), F32), vmem((8, share + coded, r1), BF16), vmem((7, share + coded, r1), BF16),
            vmem((r2, r1), BF16), vmem((r2, r1), BF16),
            pltpu.SemaphoreType.DMA((9,)), pltpu.SemaphoreType.DMA((copies,)), pltpu.SemaphoreType.DMA((copies,)),
        ],
        compiler_params=pltpu.CompilerParams(
            collective_id=0, has_side_effects=True, vmem_limit_bytes=66_000_000
        ),
    )(operator, right_test, left_test)


def solution(mesh):
    placed = (P("row", "col"), P("col", None), P("row", None))
    return jax.shard_map(
        body,
        mesh=mesh,
        in_specs=placed,
        out_specs=(P(("row", "col"), None), P("col", None)),
        check_vma=False,
    )
```

time: 308 us -> 111 us (0.36)
  the two profiles are of different devices: /device:TPU:0 before, /device:TPU:2 now
where the time goes in v1:
time: 111 us
  Pallas kernels  106 us (95%)
  local copies, waits for them, and re-layouts  3.83 us (3%)
    pallas_call x1, Pallas kernels, body(): pl.pallas_call(kernel, out_shape=(jax.ShapeDtypeStruct((share, r1), BF16)...  106 us
    unnamed x2, local copies, waits for them, and re-layouts  3.83 us

profile of v1, /device:TPU:2, one launch (start us, length us, event | category | flops | bytes accessed | tf_op | source)
XLA Modules:
  0.0 111.0 jit_solution(5919141222012753616)
XLA Ops:
  0.6 106.5 %shard_map.50 = (bf16[256,256]{1,0:T(8,128)(2,1)}, bf16[2048,256]{1,0:T(8,128)(2,1)}) custom-call(bf16[4096,2048]{1,0:T(8,128)(2,1)} %a_hbm.1, bf16[2048,256]{1,0:T(8,128)(2,1)} %r_hbm.1, bf16[4096,384]{1,0:T(8,128)(2,1)} %l_hbm.1), custom_call_target="tpu_custom_call" | custom-call | tf_op jit(solution)/shard_map/pallas_call | solution.py:313
  107.1 1.6 %copy.7 = bf16[256,256]{1,0:T(8,128)(2,1)} copy(bf16[256,256]{1,0:T(8,128)(2,1)} %get-tuple-element.4) | data formatting | bytes 262144
  108.7 2.3 %copy.8 = bf16[2048,256]{1,0:T(8,128)(2,1)} copy(bf16[2048,256]{1,0:T(8,128)(2,1)} %get-tuple-element.5) | data formatting | bytes 2097152

commit v2 on v1

--- a/solution.py
+++ b/solution.py
@@ -90,7 +90,7 @@
     a_v, r_v, l_v, lt_v, acc, lacc,
     cbuf, cd, h1, cx, h2, cy, h3, cz, g0,
     rsend, rz, rsum, ysend, ry, ag,
-    ld, lsend, lr, w_hi, w_lo,
+    ld, lsend, lx, lsum, lysend, ly, w_hi, w_lo,
     in_sem, ss, rs,
 ):
     m, n = a_hbm.shape
@@ -100,19 +100,25 @@
     z, yh = row // 2, row % 2
     yl, x, core = col // 8, (col // 2) % 4, col % 2
     y = yh * 2 + yl
-    share = 256
+    share = n // 8
+    group = 2 * share
 
     def dev(zz, yy, xx, cc):
         return (zz * 2 + yy // 2, (yy % 2) * 8 + xx * 2 + cc)
 
     chunk = m // 4
-    loads = []
+    load_l = []
     for i in range(4):
         part = pl.ds(i * chunk, chunk)
-        loads.append(pltpu.make_async_copy(l_hbm.at[part], l_v.at[part], in_sem.at[2 * i]))
-        loads.append(pltpu.make_async_copy(a_hbm.at[part], a_v.at[part], in_sem.at[2 * i + 1]))
-    loads.append(pltpu.make_async_copy(r_hbm, r_v, in_sem.at[8]))
-    for load in loads:
+        load_l.append(pltpu.make_async_copy(l_hbm.at[part], l_v.at[part], in_sem.at[i]))
+    order = (2, 1, 3, 0)
+    columns = [pl.ds(pl.multiple_of(((z + k) % 4) * group, group), group) for k in order]
+    load_a = [
+        pltpu.make_async_copy(a_hbm.at[:, here], a_v.at[:, here], in_sem.at[4 + i])
+        for i, here in enumerate(columns)
+    ]
+    load_r = pltpu.make_async_copy(r_hbm, r_v, in_sem.at[8])
+    for load in load_l + load_a + [load_r]:
         load.start()
 
     partner = dev(z, y, x, 1 - core)
@@ -140,49 +146,65 @@
         started.append(copy)
         return copy
 
-    acc[...] = jnp.zeros_like(acc)
-
     for i in range(4):
-        loads[2 * i].wait()
-        lt_v[...] = l_v[pl.ds(i * chunk, chunk), :].T
-        loads[2 * i + 1].wait()
-
-        @pl.loop(0, n // 256)
-        def _(t):
-            here = pl.ds(pl.multiple_of(t * 256, 256), 256)
-            acc[:, here] += dot(lt_v[...], a_v[pl.ds(i * chunk, chunk), here])
-
-    loads[8].wait()
-    core_part = jnp.zeros((r2, r1), F32)
-    cbuf[...] = jnp.zeros_like(cbuf)
-
-    @pl.loop(0, n // 512)
-    def _(t):
-        here = pl.ds(pl.multiple_of(t * 512, 512), 512)
-        v = acc[:, here]
+        part = pl.ds(i * chunk, chunk)
+        load_l[i].wait()
+        lt_v[:, part] = l_v[part, :].T
+
+    right_z = [None] * 4
+
+    def code_chunk(i):
+        for h in range(2):
+            store_coded(rsend.at[i, h], acc[i, :, h * share : (h + 1) * share])
+
+    def send_chunk(i):
+        k = order[i]
+        right_z[k] = push(rsend.at[i], rz.at[k - 1], z_peers[k - 1])
+
+    for i in range(4):
+        load_a[i].wait()
+        if i:
+            code_chunk(i - 1)
+        acc[i] = dot(lt_v[...], a_v[:, columns[i]])
+        if i == 0:
+            pl.semaphore_wait(barrier, 13)
+        else:
+            send_chunk(i - 1)
+
+    load_r.wait()
+    part = None
+    for i in range(4):
+        v = acc[i]
         hi = v.astype(BF16)
         v = v - hi.astype(F32)
         mid = v.astype(BF16)
         lo = (v - mid.astype(F32)).astype(BF16)
-        rt = r_v[here, :]
-        part = dot(hi, rt) + (dot(mid, rt) + dot(lo, rt))
-        cbuf[pl.ds(0, r2), :] += part[:, :128]
-        cbuf[pl.ds(r2, r2), :] += part[:, 128:]
-
-    pl.semaphore_wait(barrier, 13)
-
-    half = pl.multiple_of((1 - core) * r2, 8)
-    c_d = push(cbuf.at[pl.ds(half, r2)], cd, partner)
-
-    @pl.loop(0, 8)
-    def _(q):
-        here = pl.ds(pl.multiple_of(q * share, share), share)
-        store_coded(rsend.at[q], acc[:, here])
-
-    right_z = [
-        push(rsend.at[pl.ds(((z + k) % 4) * 2, 2)], rz.at[k - 1], z_peers[k - 1]) for k in (1, 2, 3)
-    ]
-
+        rt = r_v[columns[i], :]
+        term = dot(hi, rt) + (dot(mid, rt) + dot(lo, rt))
+        part = term if part is None else part + term
+    cbuf[pl.ds(0, r2), :] = part[:, :128]
+    cbuf[pl.ds(r2, r2), :] = part[:, 128:]
+    c_d = push(cbuf.at[pl.ds(pl.multiple_of((1 - core) * r2, 8), r2)], cd, partner)
+
+    def left_half(i):
+        @pl.loop(0, 2)
+        def _(t):
+            rows = pl.ds(pl.multiple_of((2 * i + t) * (m // 4), m // 4), m // 4)
+            product = dot(a_v[rows, :], r_v[...])
+            lacc[pl.ds(4 * i + 2 * t, 2)] = product.reshape(2, 2, m // 16, r1)
+
+        return push(lacc.at[pl.ds(4 * i, 4), 1 - core], ld.at[pl.ds(4 * i, 4)], partner)
+
+    left_x = []
+
+    def left_send(i):
+        left_d[i].wait_recv()
+        for k in (2, 1, 3):
+            q = 4 * i + (x + k) % 4
+            store_coded(lsend.at[i, k - 1], lacc[q, core] + ld[q])
+            left_x.append(push(lsend.at[i, k - 1], lx.at[i, k - 1], x_peers[k - 1]))
+
+    left_d = [left_half(0)]
     c_d.wait_recv()
     h1[...] = cbuf[pl.ds(pl.multiple_of(core * r2, 8), r2), :] + cd[...]
     n1 = r2 // 4
@@ -190,15 +212,8 @@
         push(h1.at[pl.ds(pl.multiple_of(((x + k) % 4) * n1, 8), n1)], cx.at[k - 1], x_peers[k - 1])
         for k in (1, 2, 3)
     ]
-
-    @pl.loop(0, 8)
-    def _(q):
-        rows = pl.ds(pl.multiple_of(q * 512, 512), 512)
-        part = dot(a_v[rows, :], r_v[...])
-        lacc[q, 0] = part[:256]
-        lacc[q, 1] = part[256:]
-
-    left_d = push(lacc.at[:, 1 - core], ld, partner)
+    left_d.append(left_half(1))
+    left_send(0)
 
     for copy in c_x:
         copy.wait_recv()
@@ -208,18 +223,27 @@
         push(h2.at[pl.ds(pl.multiple_of(((y + k) % 4) * n2, 8), n2)], cy.at[k - 1], y_peers[k - 1])
         for k in (1, 2, 3)
     ]
+    left_send(1)
+
     for copy in c_y:
         copy.wait_recv()
     h3[...] = h2[pl.ds(pl.multiple_of(y * n2, 8), n2), :] + (cy[0] + cy[1] + cy[2])
     cz[z] = h3[...]
     c_z = [push(h3, cz.at[z], z_peers[k - 1]) for k in (1, 2, 3)]
 
-    left_d.wait_recv()
-    me_q = yl * 4 + x
-
-    @pl.loop(0, 8)
-    def _(q):
-        store_coded(lsend.at[q], lacc[q, core] + ld[q])
+    for copy in right_z[1:]:
+        copy.wait_recv()
+
+    def right_total(h):
+        here = pl.ds(pl.multiple_of(h * share, share), share)
+        total = acc[3, :, here]
+        for k in range(3):
+            total = total + load_coded(rz.at[k, h], r2)
+        return total
+
+    store_coded(ysend, right_total(1 - yh))
+    right_y = push(ysend, ry, flip_yh)
+    rsum[...] = right_total(yh)
 
     for copy in c_z:
         copy.wait_recv()
@@ -229,39 +253,48 @@
     own = g0.at[pl.ds(base3, n2)]
     g_y = [push(own, own, y_peers[k - 1]) for k in (1, 2, 3)]
 
-    left_flip = push(lsend.at[(1 - yl) * 4 + x], lr.at[0], flip_yl)
-    left_x = [push(lsend.at[yl * 4 + (x + k) % 4], lr.at[k], x_peers[k - 1]) for k in (1, 2, 3)]
-    left_xy = [
-        push(lsend.at[(1 - yl) * 4 + (x + k) % 4], lr.at[k + 3], xy_peers[k - 1]) for k in (1, 2, 3)
-    ]
-
     for copy in g_y:
         copy.wait_recv()
     own = g0.at[pl.ds(base2, n1)]
     g_x = [push(own, own, x_peers[k - 1]) for k in (1, 2, 3)]
 
-    for copy in right_z:
-        copy.wait_recv()
-
-    @pl.loop(0, 2)
-    def _(h):
-        here = pl.ds(pl.multiple_of((z * 2 + h) * share, share), share)
-        total = acc[:, here]
-        for k in range(3):
-            total = total + load_coded(rz.at[k, h], r2)
-        rsum[h] = total
-
-    store_coded(ysend, rsum[1 - yh])
-    right_y = push(ysend, ry, flip_yh)
+    right_y.wait_recv()
+    v = (rsum[...] + load_coded(ry, r2)).T
+    half = share // 2
+    store_coded(ag.at[row, 1], v[half:])
+    store_coded(ag.at[row, 0], v[:half])
+
+    def slot(zz, yyh, which):
+        return ag.at[zz * 2 + yyh, which]
+
+    own_a, own_b = slot(z, yh, 0), slot(z, yh, 1)
+    b_z = [push(own_b, own_b, z_peers[k - 1]) for k in (1, 2, 3)]
+    a_y = push(own_a, own_a, flip_yh)
+    b_y = [push(own_b, own_b, flip_yh)]
+    a_z = [push(own_a, own_a, z_peers[k - 1]) for k in (1, 2, 3)]
 
     for copy in g_x:
         copy.wait_recv()
     own = g0.at[pl.ds(pl.multiple_of(core * r2, 8), r2)]
     g_d = push(own, own, partner)
 
-    right_y.wait_recv()
-    store_coded(ag.at[row], (rsum[yh] + load_coded(ry, r2)).T)
-    ag_y = push(ag.at[row], ag.at[row], flip_yh)
+    for copy in left_x:
+        copy.wait_recv()
+
+    def left_total(h):
+        q = 4 * h + x
+        total = lacc[q, core] + ld[q]
+        for k in range(3):
+            total = total + load_coded(lx.at[h, k], m // 16)
+        return total
+
+    store_coded(lysend, left_total(1 - yl))
+    left_y = push(lysend, ly, flip_yl)
+    lsum[...] = left_total(yl)
+
+    a_y.wait_recv()
+    next_a = slot(z, 1 - yh, 0)
+    a_z += [push(next_a, next_a, z_peers[k - 1]) for k in (1, 2, 3)]
 
     g_d.wait_recv()
     core_all = jnp.concatenate([g0[pl.ds(0, r2), :], g0[pl.ds(r2, r2), :]], axis=1)
@@ -272,27 +305,26 @@
     shift = jnp.sum(gram * eye, axis=(0, 1), keepdims=True) * 0.001 / r1
     gram = gram + shift * eye
 
-    ag_y.wait_recv()
-    both = ag.at[pl.ds(z * 2, 2)]
-    ag_z = [push(both, both, z_peers[k - 1]) for k in (1, 2, 3)]
+    for k in (3, 1, 2):
+        b_z[k - 1].wait_recv()
+        from_z = slot((z + 4 - k) % 4, yh, 1)
+        b_y.append(push(from_z, from_z, flip_yh))
 
     w = dot(core_all, inverse_256(gram), precision=HIGHEST)
     w_hi[...] = w.astype(BF16)
     w_lo[...] = (w - w_hi[...].astype(F32)).astype(BF16)
 
-    for copy in [left_flip] + left_x + left_xy:
-        copy.wait_recv()
-    total = lacc[me_q, core] + ld[me_q]
-    for k in range(7):
-        total = total + load_coded(lr.at[k], share)
-    left_out[...] = total.astype(BF16)
-
-    for copy in ag_z:
+    left_y.wait_recv()
+    left_out[...] = (lsum[...] + load_coded(ly, m // 16)).astype(BF16)
+
+    for copy in a_z:
+        copy.wait_recv()
+    for copy in b_y:
         copy.wait_recv()
 
     @pl.loop(0, 8)
     def _(q):
-        b = load_coded(ag.at[q], share)
+        b = jnp.concatenate([load_coded(ag.at[q, 0], half), load_coded(ag.at[q, 1], half)], axis=0)
         hi = b.astype(BF16)
         lo = (b - hi.astype(F32)).astype(BF16)
         v = dot(hi, w_hi[...]) + (dot(hi, w_lo[...]) + dot(lo, w_hi[...]))
@@ -302,39 +334,61 @@
         copy.wait_send()
 
 
+def store(left_v, right_v, left_hbm, right_hbm, sem):
+    copies = [
+        pltpu.make_async_copy(right_v, right_hbm, sem.at[0]),
+        pltpu.make_async_copy(left_v, left_hbm, sem.at[1]),
+    ]
+    for copy in copies:
+        copy.start()
+    for copy in copies:
+        copy.wait()
+
+
 def body(operator, right_test, left_test):
     m, n = operator.shape
     r1, r2 = right_test.shape[1], left_test.shape[1]
-    share = 256
+    left_rows, share = m // 16, n // 8
     coded = SCALE_ROWS
     vmem = pltpu.VMEM
     n1, n2 = r2 // 4, r2 // 16
-    copies = 40
-    return pl.pallas_call(
+    copies = 48
+    outs = (
+        jax.ShapeDtypeStruct((left_rows, r1), BF16),
+        jax.ShapeDtypeStruct((n, r1), BF16),
+    )
+    left, right = pl.pallas_call(
         kernel,
-        out_shape=(
-            jax.ShapeDtypeStruct((share, r1), BF16),
-            jax.ShapeDtypeStruct((n, r1), BF16),
-        ),
+        out_shape=outs,
         in_specs=[pl.BlockSpec(memory_space=pl.ANY)] * 3,
         out_specs=(pl.BlockSpec(memory_space=pltpu.VMEM),) * 2,
         scratch_shapes=[
-            vmem((m, n), BF16), vmem((n, r1), BF16), vmem((m, r2), BF16), vmem((r2, m // 4), BF16),
-            vmem((r2, n), F32), vmem((8, 2, share, r1), F32),
+            vmem((m, n), BF16), vmem((n, r1), BF16), vmem((m, r2), BF16), vmem((r2, m), BF16),
+            vmem((4, r2, n // 4), F32), vmem((8, 2, left_rows, r1), F32),
             vmem((2 * r2, 128), F32), vmem((r2, 128), F32), vmem((r2, 128), F32),
             vmem((3, n1, 128), F32), vmem((n1, 128), F32), vmem((3, n2, 128), F32),
             vmem((n2, 128), F32), vmem((4, n2, 128), F32), vmem((2 * r2, 128), F32),
-            vmem((8, r2 + coded, share), BF16), vmem((3, 2, r2 + coded, share), BF16),
-            vmem((2, r2, share), F32), vmem((r2 + coded, share), BF16), vmem((r2 + coded, share), BF16),
-            vmem((8, share + coded, r2), BF16),
-            vmem((8, share, r1), F32), vmem((8, share + coded, r1), BF16), vmem((7, share + coded, r1), BF16),
+            vmem((3, 2, r2 + coded, share), BF16), vmem((3, 2, r2 + coded, share), BF16),
+            vmem((r2, share), F32), vmem((r2 + coded, share), BF16), vmem((r2 + coded, share), BF16),
+            vmem((8, 2, share // 2 + coded, r2), BF16),
+            vmem((8, left_rows, r1), F32), vmem((2, 3, left_rows + coded, r1), BF16),
+            vmem((2, 3, left_rows + coded, r1), BF16), vmem((left_rows, r1), F32),
+            vmem((left_rows + coded, r1), BF16), vmem((left_rows + coded, r1), BF16),
             vmem((r2, r1), BF16), vmem((r2, r1), BF16),
             pltpu.SemaphoreType.DMA((9,)), pltpu.SemaphoreType.DMA((copies,)), pltpu.SemaphoreType.DMA((copies,)),
         ],
         compiler_params=pltpu.CompilerParams(
-            collective_id=0, has_side_effects=True, vmem_limit_bytes=66_000_000
+            collective_id=0, has_side_effects=True, vmem_limit_bytes=52 * 2**20
         ),
     )(operator, right_test, left_test)
+    return pl.pallas_call(
+        store,
+        out_shape=outs,
+        in_specs=[pl.BlockSpec(memory_space=pltpu.VMEM)] * 2,
+        out_specs=(pl.BlockSpec(memory_space=pl.ANY),) * 2,
+        scratch_shapes=[pltpu.SemaphoreType.DMA((2,))],
+        compiler_params=pltpu.CompilerParams(vmem_limit_bytes=4 * 2**20),
+    )(left, right)
 
 
 def solution(mesh):

time: 111 us -> 70.7 us (0.64)
  the two profiles are of different devices: /device:TPU:2 before, /device:TPU:0 now
where the time goes in v2:
time: 70.7 us; the launch traced here: 70.6 us
  Pallas kernels  69.8 us (99%)
  between operations  0.82 us (1%)
    pallas_call x1, Pallas kernels, body(): pl.pallas_call(kernel, out_shape=outs, in_specs=[pl.BlockSpec(memory_spac...  68.8 us

profile of v2, /device:TPU:0, one launch (start us, length us, event | category | flops | bytes accessed | tf_op | source)
XLA Modules:
  0.0 70.6 jit_solution(9363270453995310656)
XLA Ops:
  0.6 68.8 %shard_map.50 = (bf16[256,256]{1,0:T(8,128)(2,1)S(1)}, bf16[2048,256]{1,0:T(8,128)(2,1)S(1)}) custom-call(bf16[4096,2048]{1,0:T(8,128)(2,1)} %a_hbm.1, bf16[2048,256]{1,0:T(8,128)(2,1)} %r_hbm.1, bf16[4096,384]{1,0:T(8,128)(2,1)} %l_hbm.1), custom_call_target="tpu_custom_call" | custom-call | tf_op jit(solution)/shard_map/pallas_call | solution.py:360
  69.4 1.0 %shard_map.51 = (bf16[256,256]{1,0:T(8,128)(2,1)}, bf16[2048,256]{1,0:T(8,128)(2,1)}) custom-call(bf16[256,256]{1,0:T(8,128)(2,1)S(1)} %get-tuple-element.4.left_v, bf16[2048,256]{1,0:T(8,128)(2,1)S(1)} %get-tuple-element.5.right_v), custom_call_target="tpu_custom_call" | custom-call | tf_op jit(solution)/shard_map/pallas_call | solution.py:384

commit v3 on v2

--- a/solution.py
+++ b/solution.py
@@ -18,7 +18,7 @@
 
 
 def largest(value):
-    return jnp.maximum(jnp.max(jnp.abs(value), axis=(0, 1), keepdims=True), 1e-30)
+    return jnp.maximum(jnp.max(jnp.abs(value), axis=0, keepdims=True), 1e-30)
 
 
 def store_coded(ref, value):
@@ -35,7 +35,7 @@
 def load_coded(ref, rows):
     scale = ref[pl.ds(rows, SCALE_ROWS), :].astype(F32)[0:1, :] * (1.0 / TOP)
     y = ref[pl.ds(0, rows), :].astype(F32)
-    r = jnp.sqrt(jnp.sqrt(jnp.sqrt(jnp.abs(y)))) * scale
+    r = jnp.exp2(jnp.log2(jnp.abs(y)) * 0.125) * scale
     return jnp.where(y < 0, -r, r)
 
 
@@ -89,7 +89,7 @@
     a_hbm, r_hbm, l_hbm, left_out, right_out,
     a_v, r_v, l_v, lt_v, acc, lacc,
     cbuf, cd, h1, cx, h2, cy, h3, cz, g0,
-    rsend, rz, rsum, ysend, ry, ag,
+    terms, far, relay, rsend, rz, rsum, ysend, ry, ag,
     ld, lsend, lx, lsum, lysend, ly, w_hi, w_lo,
     in_sem, ss, rs,
 ):
@@ -151,40 +151,49 @@
         load_l[i].wait()
         lt_v[:, part] = l_v[part, :].T
 
-    right_z = [None] * 4
-
-    def code_chunk(i):
-        for h in range(2):
-            store_coded(rsend.at[i, h], acc[i, :, h * share : (h + 1) * share])
-
-    def send_chunk(i):
-        k = order[i]
-        right_z[k] = push(rsend.at[i], rz.at[k - 1], z_peers[k - 1])
+    near = [[None, None], [None, None]]
+
+    def send_far(h):
+        store_coded(far.at[h], acc[0, :, h * share : (h + 1) * share])
+        return push(far.at[h], relay.at[h], z_peers[2 * h])
+
+    def send_near(side, h, value):
+        store_coded(rsend.at[side, h], value)
+        near[side][h] = push(rsend.at[side, h], rz.at[side, h], z_peers[2 * side])
 
     for i in range(4):
         load_a[i].wait()
-        if i:
-            code_chunk(i - 1)
         acc[i] = dot(lt_v[...], a_v[:, columns[i]])
         if i == 0:
             pl.semaphore_wait(barrier, 13)
-        else:
-            send_chunk(i - 1)
-
-    load_r.wait()
-    part = None
-    for i in range(4):
+            relayed = [send_far(0), send_far(1)]
+        elif i == 1:
+            send_near(0, 1, acc[1, :, share:])
+        elif i == 2:
+            send_near(1, 0, acc[2, :, :share])
         v = acc[i]
         hi = v.astype(BF16)
         v = v - hi.astype(F32)
         mid = v.astype(BF16)
         lo = (v - mid.astype(F32)).astype(BF16)
-        rt = r_v[columns[i], :]
-        term = dot(hi, rt) + (dot(mid, rt) + dot(lo, rt))
+        terms[i, pl.ds(0, r2), :] = hi
+        terms[i, pl.ds(r2, r2), :] = mid
+        terms[i, pl.ds(2 * r2, r2), :] = lo
+
+    load_r.wait()
+    part = None
+    for i in range(4):
+        term = dot(terms[i], r_v[columns[i], :])
         part = term if part is None else part + term
+    part = part[:r2] + (part[r2 : 2 * r2] + part[2 * r2 :])
     cbuf[pl.ds(0, r2), :] = part[:, :128]
     cbuf[pl.ds(r2, r2), :] = part[:, 128:]
     c_d = push(cbuf.at[pl.ds(pl.multiple_of((1 - core) * r2, 8), r2)], cd, partner)
+
+    for copy in relayed:
+        copy.wait_recv()
+    send_near(0, 0, acc[1, :, :share] + load_coded(relay.at[0], r2))
+    send_near(1, 1, acc[2, :, share:] + load_coded(relay.at[1], r2))
 
     def left_half(i):
         @pl.loop(0, 2)
@@ -231,14 +240,14 @@
     cz[z] = h3[...]
     c_z = [push(h3, cz.at[z], z_peers[k - 1]) for k in (1, 2, 3)]
 
-    for copy in right_z[1:]:
+    for copy in near[0] + near[1]:
         copy.wait_recv()
 
     def right_total(h):
         here = pl.ds(pl.multiple_of(h * share, share), share)
         total = acc[3, :, here]
-        for k in range(3):
-            total = total + load_coded(rz.at[k, h], r2)
+        for side in range(2):
+            total = total + load_coded(rz.at[side, h], r2)
         return total
 
     store_coded(ysend, right_total(1 - yh))
@@ -322,7 +331,7 @@
     for copy in b_y:
         copy.wait_recv()
 
-    @pl.loop(0, 8)
+    @pl.loop(0, 8, unroll=2)
     def _(q):
         b = jnp.concatenate([load_coded(ag.at[q, 0], half), load_coded(ag.at[q, 1], half)], axis=0)
         hi = b.astype(BF16)
@@ -368,7 +377,8 @@
             vmem((2 * r2, 128), F32), vmem((r2, 128), F32), vmem((r2, 128), F32),
             vmem((3, n1, 128), F32), vmem((n1, 128), F32), vmem((3, n2, 128), F32),
             vmem((n2, 128), F32), vmem((4, n2, 128), F32), vmem((2 * r2, 128), F32),
-            vmem((3, 2, r2 + coded, share), BF16), vmem((3, 2, r2 + coded, share), BF16),
+            vmem((4, 3 * r2, n // 4), BF16), vmem((2, r2 + coded, share), BF16), vmem((2, r2 + coded, share), BF16),
+            vmem((2, 2, r2 + coded, share), BF16), vmem((2, 2, r2 + coded, share), BF16),
             vmem((r2, share), F32), vmem((r2 + coded, share), BF16), vmem((r2 + coded, share), BF16),
             vmem((8, 2, share // 2 + coded, r2), BF16),
             vmem((8, left_rows, r1), F32), vmem((2, 3, left_rows + coded, r1), BF16),

time: 70.7 us -> 63 us (0.89)
  Pallas kernels: 69.8 us -> 62.1 us
    pallas_call x1, Pallas kernels: 68.8 us -> 61.1 us  [body(): pl.pallas_call(kernel, out_shape=outs, in_specs=[pl.BlockSpec(memory_spac...]
where the time goes in v3:
time: 63 us; the launch traced here: 62.9 us
  Pallas kernels  62.1 us (99%)
  between operations  0.8 us (1%)
    pallas_call x1, Pallas kernels, body(): pl.pallas_call(kernel, out_shape=outs, in_specs=[pl.BlockSpec(memory_spac...  61.1 us

profile of v3, /device:TPU:0, one launch (start us, length us, event | category | flops | bytes accessed | tf_op | source)
XLA Modules:
  0.0 62.9 jit_solution(15495370572155004006)
XLA Ops:
  0.6 61.1 %shard_map.50 = (bf16[256,256]{1,0:T(8,128)(2,1)S(1)}, bf16[2048,256]{1,0:T(8,128)(2,1)S(1)}) custom-call(bf16[4096,2048]{1,0:T(8,128)(2,1)} %a_hbm.1, bf16[2048,256]{1,0:T(8,128)(2,1)} %r_hbm.1, bf16[4096,384]{1,0:T(8,128)(2,1)} %l_hbm.1), custom_call_target="tpu_custom_call" | custom-call | tf_op jit(solution)/shard_map/pallas_call | solution.py:369
  61.7 1.0 %shard_map.51 = (bf16[256,256]{1,0:T(8,128)(2,1)}, bf16[2048,256]{1,0:T(8,128)(2,1)}) custom-call(bf16[256,256]{1,0:T(8,128)(2,1)S(1)} %get-tuple-element.4.left_v, bf16[2048,256]{1,0:T(8,128)(2,1)S(1)} %get-tuple-element.5.right_v), custom_call_target="tpu_custom_call" | custom-call | tf_op jit(solution)/shard_map/pallas_call | solution.py:394
